TPU v7x, 256 devices: a whole 4x4x8 slice. The times are simulated.
256 devices in a mesh: replica: 8 (over y, core), shard: 32 (over x, z).
Axes of the slice: x: 4, y: 4, z: 8, core: 2. Of those that a mesh axis runs over, the one named last changes fastest.
Arguments:
- deltas: bfloat16 [8, 64, 128, 6144], P('replica', None, 'shard')
- block_list: int32 [8, 64], replicated, may hold values from -1 to 127, as said below
- hosting: int32 [8, 16, 8], replicated, may hold values from 0 to 1, as said below
- counts: int32 [8, 128], replicated, may hold values from 1 to 63
- params: float32 [128, 128, 6144], P('shard', 'replica'), may hold values from -6 to 6
- momentum: float32 [128, 128, 6144], P('shard', 'replica'), may hold values from -4 to 4
Outputs:
- new_params: float32 [128, 128, 6144], P('shard', 'replica')
- new_momentum: float32 [128, 128, 6144], P('shard', 'replica')
- host_params: bfloat16 [8, 64, 128, 6144], P('replica', None, 'shard')
Inputs may be any that keep to these rules, and one draw needn't show every extreme that they name: `block_list`: row r lists, each once and in any order, the blocks whose parameters replica r holds, with -1 in the other entries; block b is owned by shard b // 4, and at most 2 listed blocks of one row have the same owner. `hosting`: 1 only for blocks that appear in the replica's row of block_list.
All inputs are finite; a program needn't handle non-finite values.
Results may differ from a plain program's by a relative error of at most 0.001.
Values may be sent and summed in bfloat16 or wider, within the bound.
A program may use at most 128 MiB of HBM per device.

v0:
```python
import math
import jax
import jax.numpy as jnp
from jax import lax
from jax.sharding import Mesh
from jax.sharding import PartitionSpec as P

D = 6144
ROWS = 128
REPLICA = ("replica_0", "replica_1")
SHARD = ("shard_0", "shard_1")
REPLICA_SHARD = ("replica_0", "replica_1", "shard_0", "shard_1")
decay_rate = 0.9
outer_rate = 0.7
limit_ratio = 0.1


def by_axis(shard, axes):
    for axis in axes:
        shard = lax.psum(shard, axis)
    return shard


def slot_placement(block_lists, owned_count, capacity, shard_count):
    listed = block_lists >= 0
    owner_shard = jnp.where(listed, block_lists // owned_count, -1)
    same_owner = (owner_shard[:, :, None] == jnp.arange(shard_count)[None, None, :]).astype(
        jnp.int32
    )
    owner_rank = jnp.sum(jnp.cumsum(same_owner, axis=1) * same_owner, axis=2) - 1
    return jnp.where(listed, owner_shard * capacity + owner_rank, -1)


def per_device(deltas, block_list, hosting, counts, params, momentum):
    replicas = lax.axis_size(REPLICA)
    shard_count = lax.axis_size(SHARD)
    replica_index = lax.axis_index(REPLICA)
    shard_index = lax.axis_index(SHARD)
    slot_count = block_list.shape[1]
    capacity = slot_count // shard_count
    block_count = counts.shape[1]
    owned_count = block_count // shard_count
    local_rows = deltas.shape[2]
    owner_rows = params.shape[1]
    flat_local = deltas[0].reshape(slot_count, local_rows * D)
    weight = hosting.reshape(replicas, block_count) * counts
    totals = jnp.maximum(jnp.sum(weight, axis=0).astype(jnp.float32), 1.0)
    first_owned = shard_index * owned_count
    targets = first_owned + jnp.arange(owned_count)
    own_weight = lax.dynamic_slice_in_dim(weight, first_owned, owned_count, 1)
    own_totals = lax.dynamic_slice_in_dim(totals, first_owned, owned_count, 0)
    placement_all = slot_placement(block_list, owned_count, capacity, shard_count)
    my_place = lax.dynamic_index_in_dim(placement_all, replica_index, 0, keepdims=False)
    packing = (jnp.arange(slot_count)[:, None] == my_place[None, :]).astype(jnp.bfloat16)
    packed = jnp.dot(packing, flat_local, preferred_element_type=jnp.float32).astype(jnp.bfloat16)
    packed = packed.reshape(shard_count, capacity, local_rows, D)
    at_owner = lax.all_to_all(packed, SHARD, split_axis=0, concat_axis=2, tiled=True)
    gathered = lax.all_to_all(at_owner, REPLICA, split_axis=2, concat_axis=0, tiled=True)
    wanted = shard_index * capacity + jnp.arange(capacity)
    select = (placement_all[:, None, :] == wanted[None, :, None]).astype(jnp.int32)
    slot_block = jnp.sum(select * block_list[:, None, :], axis=2) - (1 - jnp.sum(select, axis=2))
    matches = slot_block[:, :, None] == targets[None, None, :]
    slot_weight = jnp.where(matches, own_weight[:, None, :], 0)
    mixing = slot_weight.reshape(replicas * capacity, owned_count).astype(jnp.bfloat16)
    summed = jnp.einsum(
        "sj,sx->jx",
        mixing,
        gathered.reshape(replicas * capacity, owner_rows * D),
        preferred_element_type=jnp.float32,
    )
    gradient = summed.reshape(owned_count, owner_rows, D) / own_totals[:, None, None]
    square_sum = by_axis(jnp.sum(gradient * gradient), REPLICA_SHARD)
    limit = limit_ratio * math.sqrt(block_count * ROWS * D)
    clip_factor = jnp.minimum(1.0, limit / jnp.sqrt(square_sum + 1e-06))
    scaled = clip_factor * gradient
    new_momentum = decay_rate * momentum + scaled
    new_params = params - outer_rate * (scaled + decay_rate * new_momentum)
    hosted = new_params.astype(jnp.bfloat16)
    sending = jnp.einsum(
        "rcj,jx->rcx",
        matches.astype(jnp.bfloat16),
        hosted.reshape(owned_count, owner_rows * D),
        preferred_element_type=jnp.float32,
    ).astype(jnp.bfloat16)
    sending = sending.reshape(replicas, capacity, owner_rows, D)
    returned = lax.all_to_all(
        lax.all_to_all(sending, REPLICA, split_axis=0, concat_axis=2, tiled=True),
        SHARD,
        split_axis=2,
        concat_axis=0,
        tiled=True,
    )
    host_rows = jnp.einsum(
        "pk,px->kx",
        packing,
        returned.reshape(slot_count, local_rows * D),
        preferred_element_type=jnp.float32,
    ).astype(jnp.bfloat16)
    return (new_params, new_momentum, host_rows.reshape(1, slot_count, local_rows, D))


def solution(mesh):
    finer = Mesh(mesh.devices.reshape(4, 2, 4, 8), ("replica_0", "replica_1", "shard_0", "shard_1"))
    in_specs = (
        P(REPLICA, None, SHARD, None),
        P(),
        P(),
        P(),
        P(SHARD, REPLICA, None),
        P(SHARD, REPLICA, None),
    )
    out_specs = (P(SHARD, REPLICA, None), P(SHARD, REPLICA, None), P(REPLICA, None, SHARD, None))
    return jax.shard_map(
        per_device, mesh=finer, in_specs=in_specs, out_specs=out_specs, check_vma=False
    )
```

profile of v0, /device:TPU:8, one launch (start us, length us, event | category | flops | bytes accessed | tf_op | source)
XLA Modules:
  0.0 331.8 jit_solution(15116666798434059264)
XLA Ops:
  0.6 0.8 copy.72
  1.4 1.3 fusion.15
  2.8 3.7 %copy.97 = bf16[8,8,4,6144]{3,1,2,0:T(8,128)(2,1)S(1)} copy(bf16[8,8,4,6144]{3,2,1,0:T(4,128)(2,1)} %bitcast.58) | data formatting | bytes 6291456
  6.5 0.2 dynamic-slice_reduce_fusion
  6.7 2.6 convolution_convert_fusion.2
  9.3 4.1 %reshape.102 = bf16[32,2,4,6144]{3,2,1,0:T(4,128)(2,1)S(1)} reshape(bf16[64,24576]{1,0:T(8,128)(2,1)} %convolution_convert_fusion.2) | data formatting | bytes 6291456 | tf_op jit(solution)/shard_map/reshape | solution.py:56
  13.5 3.2 copy.80
  16.7 84.9 %all_to_all.66 = bf16[32,2,4,6144]{3,1,2,0:T(2,128)(2,1)} all-to-all(bf16[32,2,4,6144]{3,1,2,0:T(2,128)(2,1)S(1)} %copy.80), channel_id=1, replica_groups=mesh['replica_0'=4,'replica_1'=2,'shard_0'=4,'shard_1'=8] {'shard_0','sh..., dimensions={0} | all-to-all | bytes 6291456 | tf_op jit(solution)/shard_map/all_to_all | solution.py:57
  101.5 0.0 copy-start.4
  101.5 0.0 copy-start.3
  101.6 0.0 copy-start.5
  101.6 5.0 %all-to-all-start.1 = ((bf16[1,2,128,6144]{3,1,0,2:T(2,128)(2,1)}), bf16[1,2,128,6144]{3,1,0,2:T(2,128)(2,1)S(1)}, u32[]{:S(2)}, u32[]{:S(2)}) async-start(bf16[1,2,128,6144]{3,1,0,2:T(2,128)(2,1)} %bitcast.50), calls=%async_computation.1 | async-start | bytes 6291456 | tf_op jit(solution)/shard_map/all_to_all | solution.py:58
  106.6 0.1 copy.77
  106.7 0.0 copy-done.4
  106.7 0.2 fusion.11
  106.9 0.1 copy.78
  107.0 0.0 copy-done.3
  107.0 0.1 copy.79
  107.1 0.1 reshape.101
  107.2 0.0 copy-done.5
  107.2 0.1 dynamic_slice.12
  107.3 0.1 constant_dynamic-slice_fusion
  107.4 0.1 select_convert_fusion
  107.4 36.1 %all-to-all-done.1 = bf16[1,2,128,6144]{3,1,0,2:T(2,128)(2,1)S(1)} async-done(((bf16[1,2,128,6144]{3,1,0,2:T(2,128)(2,1)}), bf16[1,2,128,6144]{3,1,0,2:T(2,128)(2,1)S(1)}, u32[]{:S(2)}, u32[]{:S(2)}) %all-to-all-start.1) | async-done | bytes 3145760 | tf_op jit(solution)/shard_map/all_to_all | solution.py:58
  143.5 1.1 copy.82
  144.6 0.0 copy-start.1
  144.6 0.0 copy-start.2
  144.7 5.2 %multiply_reduce_fusion = (f32[]{:T(128)}, f32[4,16,6144]{2,0,1:T(4,128)}) fusion(f32[4]{0:T(128)S(1)} %dynamic_slice.12, bf16[16,4,1]{1,0,2:T(8,128)(2,1)S(1)} %bitcast.60, bf16[2,8,16,6144]{3,2,1,0:T(8,128)(2,1)S(1)} %bitcast.59), kind=kOutput, calls=%fused_computation.9 | convolution fusion | flops 13762559 | bytes 4718740 | tf_op jit(solution)/shard_map/sj,sx->jx/dot_general | solution.py:65
  149.8 9.8 %psum.28 = f32[]{:T(128)} all-reduce(f32[]{:T(128)} %get-tuple-element.27), channel_id=1, replica_groups=mesh['replica_0'=4,'replica_1'=2,'shard_0'=4,'shard_1'=8] {'replica_0'}, use_global_device_ids=true, to_apply=%region_6.7 | all-reduce | flops 1 | bytes 8 | tf_op jit(solution)/shard_map/psum | solution.py:20
  159.6 3.1 psum.29
  162.7 9.1 %psum.30 = f32[]{:T(128)} all-reduce(f32[]{:T(128)} %psum.29), channel_id=1, replica_groups=mesh['replica_0'=4,'replica_1'=2,'shard_0'=4,'shard_1'=8] {'shard_0'}, use_global_device_ids=true, to_apply=%region_8.9 | all-reduce | flops 1 | bytes 8 | tf_op jit(solution)/shard_map/psum | solution.py:20
  171.8 16.8 %psum.31 = f32[]{:T(128)} all-reduce(f32[]{:T(128)} %psum.30), channel_id=1, replica_groups=mesh['replica_0'=4,'replica_1'=2,'shard_0'=4,'shard_1'=8] {'shard_1'}, use_global_device_ids=true, to_apply=%region_9.10 | all-reduce | flops 1 | bytes 8 | tf_op jit(solution)/shard_map/psum | solution.py:20
  189.4 0.0 copy-done.1
  189.4 0.0 copy-done.2
  189.4 6.0 %fusion.13 = (bf16[4,16,6144]{2,0,1:T(4,128)(2,1)S(1)}, f32[4,16,6144]{2,0,1:T(4,128)}, f32[4,16,6144]{2,0,1:T(4,128)}) fusion(f32[4,16,6144]{2,1,0:T(8,128)S(1)} %copy-done.1, f32[4,16,6144]{2,0,1:T(4,128)} %get-tuple-element.28, f32[]{:T(128)S(6)} %min.3, f32[4,16,6144]{2,1,0:T(8,128)S(1)} %copy-done.2), kind=kLoop, calls=%fused_computation.40 | loop fusion | flops 3145728 | bytes 8650756 | tf_op jit(solution)/shard_map/convert_element_type | solution.py:78
  195.3 1.0 convolution_convert_fusion
  196.3 1.7 copy.88
  198.0 41.0 %all_to_all.67 = bf16[8,2,16,6144]{3,2,1,0:T(8,128)(2,1)S(1)} all-to-all(bf16[8,2,16,6144]{3,2,1,0:T(8,128)(2,1)S(1)} %copy.88), channel_id=1, replica_groups=mesh['replica_0'=4,'replica_1'=2,'shard_0'=4,'shard_1'=8] {'replica_0','..., dimensions={0} | all-to-all | bytes 6291456 | tf_op jit(solution)/shard_map/all_to_all | solution.py:87
  239.0 0.2 copy.89
  239.2 4.9 %copy.90 = bf16[1,2,128,6144]{3,1,0,2:T(2,128)(2,1)} copy(bf16[1,2,128,6144]{3,2,1,0:T(8,128)(2,1)S(1)} %bitcast.55) | data formatting | bytes 6291456 | tf_op jit(solution)/shard_map/all_to_all | solution.py:87
  244.1 5.3 %all-to-all-start.3 = ((bf16[1,2,128,6144]{3,1,0,2:T(2,128)(2,1)}), bf16[1,2,128,6144]{3,1,0,2:T(2,128)(2,1)S(1)}, u32[]{:S(2)}, u32[]{:S(2)}) async-start(bf16[1,2,128,6144]{3,1,0,2:T(2,128)(2,1)} %copy.90), calls=%async_computation.3 | async-start | bytes 6291456 | tf_op jit(solution)/shard_map/all_to_all | solution.py:86
  249.5 0.0 copy-start
  249.5 3.6 %copy.92 = f32[4,16,6144]{2,1,0:T(8,128)} copy(f32[4,16,6144]{2,0,1:T(4,128)} %get-tuple-element.21) | data formatting | bytes 3145728
  253.1 0.0 copy-done
  253.1 2.1 copy.93
  255.1 68.6 %all-to-all-done.3 = bf16[1,2,128,6144]{3,1,0,2:T(2,128)(2,1)S(1)} async-done(((bf16[1,2,128,6144]{3,1,0,2:T(2,128)(2,1)}), bf16[1,2,128,6144]{3,1,0,2:T(2,128)(2,1)S(1)}, u32[]{:S(2)}, u32[]{:S(2)}) %all-to-all-start.3) | async-done | bytes 3145760 | tf_op jit(solution)/shard_map/all_to_all | solution.py:86
  323.7 1.6 copy.91
  325.3 1.8 copy.99
  327.2 1.0 convolution_convert_fusion.1
  328.2 3.6 %reshape.107 = bf16[1,64,4,6144]{3,2,1,0:T(4,128)(2,1)} reshape(bf16[64,24576]{1,0:T(8,128)(2,1)S(1)} %convolution_convert_fusion.1) | data formatting | bytes 6291456 | tf_op jit(solution)/shard_map/reshape | solution.py:99
  (7 shorter events, 0.1 us)
Async XLA Ops:
  101.5 5.1 %copy-start.4 = (s32[8,64]{1,0:T(8,128)S(1)}, s32[8,64]{1,0:T(8,128)}, u32[]{:S(2)}) copy-start(s32[8,64]{1,0:T(8,128)} %param.7) | copy-start | bytes 6148
  101.5 5.4 %copy-start.3 = (s32[8,16,8]{1,2,0:T(8,128)S(1)}, s32[8,16,8]{1,2,0:T(8,128)}, u32[]{:S(2)}) copy-start(s32[8,16,8]{1,2,0:T(8,128)} %param.8) | copy-start | bytes 12292
  101.6 5.6 %copy-start.5 = (s32[8,128]{1,0:T(8,128)S(1)}, s32[8,128]{1,0:T(8,128)}, u32[]{:S(2)}) copy-start(s32[8,128]{1,0:T(8,128)} %param.9) | copy-start | bytes 12292
  101.6 42.0 %all-to-all-start.1 = ((bf16[1,2,128,6144]{3,1,0,2:T(2,128)(2,1)}), bf16[1,2,128,6144]{3,1,0,2:T(2,128)(2,1)S(1)}, u32[]{:S(2)}, u32[]{:S(2)}) async-start(bf16[1,2,128,6144]{3,1,0,2:T(2,128)(2,1)} %bitcast.50), calls=%async_computation.1 | async-start | bytes 6291456 | tf_op jit(solution)/shard_map/all_to_all | solution.py:58
  144.6 44.7 %copy-start.1 = (f32[4,16,6144]{2,1,0:T(8,128)S(1)}, f32[4,16,6144]{2,1,0:T(8,128)}, u32[]{:S(2)}) copy-start(f32[4,16,6144]{2,1,0:T(8,128)} %param.11) | copy-start | bytes 4718596
  144.6 44.7 %copy-start.2 = (f32[4,16,6144]{2,1,0:T(8,128)S(1)}, f32[4,16,6144]{2,1,0:T(8,128)}, u32[]{:S(2)}) copy-start(f32[4,16,6144]{2,1,0:T(8,128)} %param.10) | copy-start | bytes 4718596
  244.1 79.6 %all-to-all-start.3 = ((bf16[1,2,128,6144]{3,1,0,2:T(2,128)(2,1)}), bf16[1,2,128,6144]{3,1,0,2:T(2,128)(2,1)S(1)}, u32[]{:S(2)}, u32[]{:S(2)}) async-start(bf16[1,2,128,6144]{3,1,0,2:T(2,128)(2,1)} %copy.90), calls=%async_computation.3 | async-start | bytes 6291456 | tf_op jit(solution)/shard_map/all_to_all | solution.py:86
  249.5 3.6 %copy-start = (f32[4,16,6144]{2,0,1:T(4,128)S(1)}, f32[4,16,6144]{2,0,1:T(4,128)}, u32[]{:S(2)}) copy-start(f32[4,16,6144]{2,0,1:T(4,128)} %get-tuple-element.26) | copy-start | bytes 4718596
where the time goes:
time: 332 us
  blocking collectives  165 us (50%)
  waiting for transfers between devices  105 us (32%)
  local copies, waits for them, and re-layouts  33.1 us (10%)
  starting transfers between devices  10.3 us (3%)
  matrix products  9.8 us (3%)
  other arithmetic  7.66 us (2%)
    all_to_all x1, blocking collectives, per_device(): lax.all_to_all(packed, SHARD, split_axis=0, concat_axis=2, tiled=True)  84.9 us
    all_to_all x1, waiting for transfers between devices, per_device(): lax.all_to_all(lax.all_to_all(sending, REPLICA, split_axis=0, concat_axis...  68.6 us
    all_to_all x1, blocking collectives, per_device(): lax.all_to_all(sending, REPLICA, split_axis=0, concat_axis=2, tiled=True)  41 us
    psum x4, blocking collectives, by_axis(): shard = lax.psum(shard, axis)  38.8 us
    all_to_all x1, waiting for transfers between devices, per_device(): lax.all_to_all(at_owner, REPLICA, split_axis=2, concat_axis=0, tiled=True)  36.1 us
    unnamed x18, local copies, waits for them, and re-layouts  12 us
    reshape x2, local copies, waits for them, and re-layouts, per_device(): packed = packed.reshape(shard_count, capacity, local_rows, D)  7.37 us
  transfers between devices with their start and end apart: 2, of which 2 were waited for; matrix products, arithmetic and copies ran while one was open for 2% of the time, Pallas kernels for 0%

commit v1 on v0

--- a/solution.py
+++ b/solution.py
@@ -17,7 +17,7 @@
 
 def by_axis(shard, axes):
     for axis in axes:
-        shard = lax.psum(shard, axis)
+        shard = jnp.sum(lax.all_gather(shard, axis), axis=0)
     return shard
 
 

time: 332 us -> 340 us (1.024)
  local copies, waits for them, and re-layouts: 33.1 us -> 41 us
    psum x4 -> x0, blocking collectives: 38.8 us -> none  [by_axis(): shard = lax.psum(shard, axis)]
    unnamed x0 -> x4, blocking collectives: none -> 36.3 us
    unnamed x18 -> x38, local copies, waits for them, and re-layouts: 12 us -> 20 us
where the time goes in v1:
time: 340 us; the launch traced here: 339 us
  blocking collectives  162 us (48%)
  waiting for transfers between devices  104 us (31%)
  local copies, waits for them, and re-layouts  41 us (12%)
  starting transfers between devices  10.4 us (3%)
  other arithmetic  10.1 us (3%)
  matrix products  9.8 us (3%)
    all_to_all x1, blocking collectives, per_device(): lax.all_to_all(packed, SHARD, split_axis=0, concat_axis=2, tiled=True)  84.9 us
    all_to_all x1, waiting for transfers between devices, per_device(): lax.all_to_all(lax.all_to_all(sending, REPLICA, split_axis=0, concat_axis...  68.6 us
    all_to_all x1, blocking collectives, per_device(): lax.all_to_all(sending, REPLICA, split_axis=0, concat_axis=2, tiled=True)  41 us
    unnamed x4, blocking collectives  36.3 us
    all_to_all x1, waiting for transfers between devices, per_device(): lax.all_to_all(at_owner, REPLICA, split_axis=2, concat_axis=0, tiled=True)  35.5 us
    unnamed x38, local copies, waits for them, and re-layouts  20 us
    reshape x2, local copies, waits for them, and re-layouts, per_device(): packed = packed.reshape(shard_count, capacity, local_rows, D)  7.37 us
  transfers between devices with their start and end apart: 2, of which 2 were waited for; matrix products, arithmetic and copies ran while one was open for 2% of the time, Pallas kernels for 0%

profile of v1, /device:TPU:8, one launch (start us, length us, event | category | flops | bytes accessed | tf_op | source)
XLA Modules:
  0.0 339.1 jit_solution(3412133086456763877)
XLA Ops:
  0.6 0.8 copy.72
  1.4 1.3 fusion.15
  2.8 3.7 %copy.97 = bf16[8,8,4,6144]{3,1,2,0:T(8,128)(2,1)S(1)} copy(bf16[8,8,4,6144]{3,2,1,0:T(4,128)(2,1)} %bitcast.66) | data formatting | bytes 6291456
  6.5 0.2 dynamic-slice_reduce_fusion
  6.7 2.6 convolution_convert_fusion.2
  9.3 4.1 %reshape.102 = bf16[32,2,4,6144]{3,2,1,0:T(4,128)(2,1)S(1)} reshape(bf16[64,24576]{1,0:T(8,128)(2,1)} %convolution_convert_fusion.2) | data formatting | bytes 6291456 | tf_op jit(solution)/shard_map/reshape | solution.py:56
  13.5 3.2 copy.80
  16.7 84.9 %all_to_all.66 = bf16[32,2,4,6144]{3,1,2,0:T(2,128)(2,1)} all-to-all(bf16[32,2,4,6144]{3,1,2,0:T(2,128)(2,1)S(1)} %copy.80), channel_id=1, replica_groups=mesh['replica_0'=4,'replica_1'=2,'shard_0'=4,'shard_1'=8] {'shard_0','sh..., dimensions={0} | all-to-all | bytes 6291456 | tf_op jit(solution)/shard_map/all_to_all | solution.py:57
  101.6 5.1 %all-to-all-start.1 = ((bf16[1,2,128,6144]{3,1,0,2:T(2,128)(2,1)}), bf16[1,2,128,6144]{3,1,0,2:T(2,128)(2,1)S(1)}, u32[]{:S(2)}, u32[]{:S(2)}) async-start(bf16[1,2,128,6144]{3,1,0,2:T(2,128)(2,1)} %bitcast.58), calls=%async_computation.1 | async-start | bytes 6291456 | tf_op jit(solution)/shard_map/all_to_all | solution.py:58
  106.6 0.1 copy.77
  106.7 0.0 copy-done.4
  106.7 0.2 fusion.11
  106.9 0.1 copy.78
  107.0 0.0 copy-done.3
  107.0 0.1 copy.79
  107.1 0.1 reshape.101
  107.2 0.0 copy-done.9
  107.2 0.6 dynamic-slice
  107.8 0.0 copy-done.5
  107.8 0.1 dynamic_slice.12
  107.9 0.1 constant_dynamic-slice_fusion
  108.0 0.1 select_convert_fusion
  108.0 35.5 %all-to-all-done.1 = bf16[1,2,128,6144]{3,1,0,2:T(2,128)(2,1)S(1)} async-done(((bf16[1,2,128,6144]{3,1,0,2:T(2,128)(2,1)}), bf16[1,2,128,6144]{3,1,0,2:T(2,128)(2,1)S(1)}, u32[]{:S(2)}, u32[]{:S(2)}) %all-to-all-start.1) | async-done | bytes 3145760 | tf_op jit(solution)/shard_map/all_to_all | solution.py:58
  143.6 1.1 copy.82
  144.7 0.0 copy-start.8
  144.7 0.0 copy-start.7
  144.7 0.0 copy-start.6
  144.7 0.0 copy-start.1
  144.7 0.0 copy-start.2
  144.7 5.2 %multiply_reduce_fusion = (f32[]{:T(128)}, f32[4,16,6144]{2,0,1:T(4,128)}) fusion(f32[4]{0:T(128)S(1)} %dynamic_slice.12, bf16[16,4,1]{1,0,2:T(8,128)(2,1)S(1)} %bitcast.68, bf16[2,8,16,6144]{3,2,1,0:T(8,128)(2,1)S(1)} %bitcast.67), kind=kOutput, calls=%fused_computation.9 | convolution fusion | flops 13762559 | bytes 4718740 | tf_op jit(solution)/shard_map/sj,sx->jx/dot_general | solution.py:65
  149.9 1.4 dynamic-update-slice
  151.3 0.0 copy-done.8
  151.3 0.6 dynamic-slice.1
  151.9 9.2 %all-reduce = f32[4]{0:T(128)S(1)} all-reduce(f32[4]{0:T(128)S(1)} %dynamic-update-slice), channel_id=1, replica_groups=mesh['replica_0'=4,'replica_1'=2,'shard_0'=4,'shard_1'=8] {'replica_0'}, use_global_device_ids=true, to_apply=%add | all-reduce | flops 4 | bytes 32
  161.0 0.6 reduce_sum.86
  161.6 1.4 dynamic-update-slice.1
  163.0 0.0 copy-done.7
  163.1 0.6 dynamic-slice.2
  163.6 2.4 all-reduce.1
  166.1 0.6 reduce_sum.87
  166.7 1.4 dynamic-update-slice.2
  168.1 0.0 copy-done.6
  168.1 0.6 dynamic-slice.3
  168.7 8.5 %all-reduce.2 = f32[4]{0:T(128)S(1)} all-reduce(f32[4]{0:T(128)S(1)} %dynamic-update-slice.2), channel_id=1, replica_groups=mesh['replica_0'=4,'replica_1'=2,'shard_0'=4,'shard_1'=8] {'shard_0'}, use_global_device_ids=true, to_apply=%add.2 | all-reduce | flops 4 | bytes 32
  177.2 0.6 reduce_sum.88
  177.8 1.4 dynamic-update-slice.3
  179.2 16.2 %all-reduce.3 = f32[8]{0:T(128)S(1)} all-reduce(f32[8]{0:T(128)S(1)} %dynamic-update-slice.3), channel_id=1, replica_groups=mesh['replica_0'=4,'replica_1'=2,'shard_0'=4,'shard_1'=8] {'shard_1'}, use_global_device_ids=true, to_apply=%add.3 | all-reduce | flops 8 | bytes 64
  195.4 0.6 reduce_sum.89
  196.7 0.0 copy-done.1
  196.7 6.0 %fusion.13 = (bf16[4,16,6144]{2,0,1:T(4,128)(2,1)S(1)}, f32[4,16,6144]{2,0,1:T(4,128)}, f32[4,16,6144]{2,0,1:T(4,128)}) fusion(f32[4,16,6144]{2,1,0:T(8,128)S(1)} %copy-done.1, f32[4,16,6144]{2,0,1:T(4,128)} %get-tuple-element.28, f32[]{:T(128)S(6)} %min.3, f32[4,16,6144]{2,1,0:T(8,128)S(1)} %copy-done.2), kind=kLoop, calls=%fused_computation.40 | loop fusion | flops 3145728 | bytes 8650756 | tf_op jit(solution)/shard_map/convert_element_type | solution.py:78
  202.6 1.0 convolution_convert_fusion
  203.6 1.7 copy.88
  205.3 41.0 %all_to_all.67 = bf16[8,2,16,6144]{3,2,1,0:T(8,128)(2,1)S(1)} all-to-all(bf16[8,2,16,6144]{3,2,1,0:T(8,128)(2,1)S(1)} %copy.88), channel_id=1, replica_groups=mesh['replica_0'=4,'replica_1'=2,'shard_0'=4,'shard_1'=8] {'replica_0','..., dimensions={0} | all-to-all | bytes 6291456 | tf_op jit(solution)/shard_map/all_to_all | solution.py:87
  246.3 0.2 copy.89
  246.6 4.9 %copy.90 = bf16[1,2,128,6144]{3,1,0,2:T(2,128)(2,1)} copy(bf16[1,2,128,6144]{3,2,1,0:T(8,128)(2,1)S(1)} %bitcast.63) | data formatting | bytes 6291456 | tf_op jit(solution)/shard_map/all_to_all | solution.py:87
  251.5 5.3 %all-to-all-start.3 = ((bf16[1,2,128,6144]{3,1,0,2:T(2,128)(2,1)}), bf16[1,2,128,6144]{3,1,0,2:T(2,128)(2,1)S(1)}, u32[]{:S(2)}, u32[]{:S(2)}) async-start(bf16[1,2,128,6144]{3,1,0,2:T(2,128)(2,1)} %copy.90), calls=%async_computation.3 | async-start | bytes 6291456 | tf_op jit(solution)/shard_map/all_to_all | solution.py:86
  256.8 3.6 %copy.92 = f32[4,16,6144]{2,1,0:T(8,128)} copy(f32[4,16,6144]{2,0,1:T(4,128)} %get-tuple-element.21) | data formatting | bytes 3145728
  260.4 0.0 copy-done
  260.4 2.1 copy.93
  262.4 68.6 %all-to-all-done.3 = bf16[1,2,128,6144]{3,1,0,2:T(2,128)(2,1)S(1)} async-done(((bf16[1,2,128,6144]{3,1,0,2:T(2,128)(2,1)}), bf16[1,2,128,6144]{3,1,0,2:T(2,128)(2,1)S(1)}, u32[]{:S(2)}, u32[]{:S(2)}) %all-to-all-start.3) | async-done | bytes 3145760 | tf_op jit(solution)/shard_map/all_to_all | solution.py:86
  331.0 1.6 copy.91
  332.6 1.8 copy.99
  334.5 1.0 convolution_convert_fusion.1
  335.5 3.6 %reshape.107 = bf16[1,64,4,6144]{3,2,1,0:T(4,128)(2,1)} reshape(bf16[64,24576]{1,0:T(8,128)(2,1)S(1)} %convolution_convert_fusion.1) | data formatting | bytes 6291456 | tf_op jit(solution)/shard_map/reshape | solution.py:99
  (17 shorter events, 0.1 us)
Async XLA Ops:
  101.5 5.1 %copy-start.4 = (s32[8,64]{1,0:T(8,128)S(1)}, s32[8,64]{1,0:T(8,128)}, u32[]{:S(2)}) copy-start(s32[8,64]{1,0:T(8,128)} %param.7) | copy-start | bytes 6148
  101.5 5.4 %copy-start.3 = (s32[8,16,8]{1,2,0:T(8,128)S(1)}, s32[8,16,8]{1,2,0:T(8,128)}, u32[]{:S(2)}) copy-start(s32[8,16,8]{1,2,0:T(8,128)} %param.8) | copy-start | bytes 12292
  101.6 5.6 %copy-start.9 = (u32[256]{0:T(256)S(1)}, u32[256]{0:T(256)}, u32[]{:S(2)}) copy-start(u32[256]{0:T(256)} %constant.74) | copy-start | bytes 3076
  101.6 6.2 %copy-start.5 = (s32[8,128]{1,0:T(8,128)S(1)}, s32[8,128]{1,0:T(8,128)}, u32[]{:S(2)}) copy-start(s32[8,128]{1,0:T(8,128)} %param.9) | copy-start | bytes 12292
  101.6 42.0 %all-to-all-start.1 = ((bf16[1,2,128,6144]{3,1,0,2:T(2,128)(2,1)}), bf16[1,2,128,6144]{3,1,0,2:T(2,128)(2,1)S(1)}, u32[]{:S(2)}, u32[]{:S(2)}) async-start(bf16[1,2,128,6144]{3,1,0,2:T(2,128)(2,1)} %bitcast.58), calls=%async_computation.1 | async-start | bytes 6291456 | tf_op jit(solution)/shard_map/all_to_all | solution.py:58
  144.7 6.6 %copy-start.8 = (u32[256]{0:T(256)S(1)}, u32[256]{0:T(256)}, u32[]{:S(2)}) copy-start(u32[256]{0:T(256)} %constant.79) | copy-start | bytes 3076
  144.7 18.4 %copy-start.7 = (u32[256]{0:T(256)S(1)}, u32[256]{0:T(256)}, u32[]{:S(2)}) copy-start(u32[256]{0:T(256)} %constant.84) | copy-start | bytes 3076
  144.7 23.4 %copy-start.6 = (u32[256]{0:T(256)S(1)}, u32[256]{0:T(256)}, u32[]{:S(2)}) copy-start(u32[256]{0:T(256)} %constant.89) | copy-start | bytes 3076
  144.7 52.0 %copy-start.1 = (f32[4,16,6144]{2,1,0:T(8,128)S(1)}, f32[4,16,6144]{2,1,0:T(8,128)}, u32[]{:S(2)}) copy-start(f32[4,16,6144]{2,1,0:T(8,128)} %param.11) | copy-start | bytes 4718596
  144.7 52.0 %copy-start.2 = (f32[4,16,6144]{2,1,0:T(8,128)S(1)}, f32[4,16,6144]{2,1,0:T(8,128)}, u32[]{:S(2)}) copy-start(f32[4,16,6144]{2,1,0:T(8,128)} %param.10) | copy-start | bytes 4718596
  251.5 79.6 %all-to-all-start.3 = ((bf16[1,2,128,6144]{3,1,0,2:T(2,128)(2,1)}), bf16[1,2,128,6144]{3,1,0,2:T(2,128)(2,1)S(1)}, u32[]{:S(2)}, u32[]{:S(2)}) async-start(bf16[1,2,128,6144]{3,1,0,2:T(2,128)(2,1)} %copy.90), calls=%async_computation.3 | async-start | bytes 6291456 | tf_op jit(solution)/shard_map/all_to_all | solution.py:86
  256.8 3.6 %copy-start = (f32[4,16,6144]{2,0,1:T(4,128)S(1)}, f32[4,16,6144]{2,0,1:T(4,128)}, u32[]{:S(2)}) copy-start(f32[4,16,6144]{2,0,1:T(4,128)} %get-tuple-element.26) | copy-start | bytes 4718596
